TPU v7x, 32 devices: a whole 2x2x4 slice. The times are simulated.
32 devices in a mesh: hot: 4 (over z), cold: 8 (over y, x, core).
Axes of the slice: x: 2, y: 2, z: 4, core: 2. Of those that a mesh axis runs over, the one named last changes fastest.
Arguments:
- tokens: bfloat16 [128, 8192], P('cold', 'hot'), may hold values from -6 to 6
- hot_gate: bfloat16 [8192, 1024], P('hot', 'cold'), may hold values from -0.0625 to 0.0625
- hot_up: bfloat16 [8192, 1024], P('hot', 'cold'), may hold values from -0.0625 to 0.0625
- hot_down: bfloat16 [1024, 8192], P('cold', 'hot'), may hold values from -0.125 to 0.125
- cold_gate: bfloat16 [8192, 6144], P('hot', 'cold'), may hold values from -0.0625 to 0.0625
- cold_up: bfloat16 [8192, 6144], P('hot', 'cold'), may hold values from -0.0625 to 0.0625
- cold_down: bfloat16 [6144, 8192], P('cold', 'hot'), may hold values from -0.125 to 0.125
- hot_ids: int32 [8], replicated, may hold values from 0 to 55, as said below
- cold_ids: int32 [48], replicated, may hold values from 0 to 55, as said below
- block_mask: int32 [128, 56], replicated, may hold values from 0 to 1, as said below
Outputs:
- mixed: bfloat16 [128, 8192], P('cold', 'hot')
Inputs may be any that keep to these rules, and one draw needn't show every extreme that they name: hot_ids and cold_ids together name every block number from 0 to 55 once. `cold_ids`: cold slot s lies with index s // 6 of cold. `block_mask`: among the 16 tokens of one index of cold, at most 8 have a 1 in a cold slot of one given index of cold; in every draw some index of cold gets exactly 8 such tokens from every index of cold.
All inputs are finite; a program needn't handle non-finite values.
Results may differ from a plain program's by a relative error of at most 0.0049.
Values may be sent and summed in bfloat16 or wider, within the bound.
A program may use at most 64 MiB of HBM per device.

v0:
```python
import jax
import jax.numpy as jnp
from jax import lax
from jax.sharding import PartitionSpec as P

BLOCK = 128


def expand_bits(block_bits):
    row_total = block_bits.shape[0]
    widened = jnp.broadcast_to(
        block_bits.astype(jnp.float32)[:, :, None], (row_total, block_bits.shape[1], BLOCK)
    )
    return widened.reshape(row_total, block_bits.shape[1] * BLOCK)


def gated_hidden(gate_sum, up_sum, block_bits):
    return (jax.nn.silu(gate_sum) * up_sum * expand_bits(block_bits)).astype(jnp.bfloat16)


def body(
    tokens, hot_gate, hot_up, hot_down, cold_gate, cold_up, cold_down, hot_ids, cold_ids, block_mask
):
    groups = lax.axis_size("cold")
    own_group = lax.axis_index("cold")
    local_rows = tokens.shape[0]
    slot_count = local_rows // 2
    all_rows = block_mask.shape[0]
    feature_cols = tokens.shape[1]
    hot_width = hot_gate.shape[1]
    hot_blocks = hot_width // BLOCK
    cold_blocks = cold_gate.shape[1] // BLOCK
    slot_rows = groups * slot_count
    cold_bits = jnp.take(block_mask, cold_ids, axis=1)
    group_hits = jnp.max(cold_bits.reshape(all_rows, groups, cold_blocks), axis=2)
    source_hits = group_hits.reshape(groups, local_rows, groups)
    slot_index = jnp.cumsum(source_hits, axis=1) - source_hits
    my_hits = lax.dynamic_index_in_dim(source_hits, own_group, 0, keepdims=False)
    my_slots = lax.dynamic_index_in_dim(slot_index, own_group, 0, keepdims=False)
    slot_range = jnp.arange(slot_count, dtype=jnp.int32)
    chosen = (my_slots.T[:, None, :] == slot_range[None, :, None]) & (my_hits.T[:, None, :] > 0)
    chosen = chosen.astype(jnp.bfloat16)
    outgoing = jnp.einsum("gst,td->gsd", chosen, tokens, preferred_element_type=jnp.float32).astype(
        jnp.bfloat16
    )
    arrived = lax.all_to_all(outgoing, "cold", split_axis=0, concat_axis=0, tiled=True)
    arrived = arrived.reshape(slot_rows, feature_cols)
    own_hits = lax.dynamic_index_in_dim(source_hits, own_group, 2, keepdims=False)
    own_slots = lax.dynamic_index_in_dim(slot_index, own_group, 2, keepdims=False)
    source_base = jnp.arange(groups, dtype=jnp.int32)[:, None] * slot_count
    target = jnp.where(own_hits > 0, source_base + own_slots, slot_rows).reshape(all_rows)
    row_token = (
        jnp.full((slot_rows + 1,), all_rows, jnp.int32)
        .at[target]
        .set(jnp.arange(all_rows, dtype=jnp.int32))[:slot_rows]
    )
    own_bits = lax.dynamic_slice_in_dim(cold_bits, own_group * cold_blocks, cold_blocks, 1)
    padded_bits = jnp.concatenate([own_bits, jnp.zeros((1, cold_blocks), own_bits.dtype)], axis=0)
    arrived_bits = jnp.take(padded_bits, row_token, axis=0)
    my_hot = lax.dynamic_slice_in_dim(hot_ids, own_group * hot_blocks, hot_blocks, 0)
    hot_bits = jnp.take(block_mask, my_hot, axis=1)
    both_hot = jnp.concatenate([hot_gate, hot_up], axis=1)
    hot_parts = jnp.dot(
        lax.all_gather(tokens, "cold", axis=0, tiled=True),
        both_hot,
        preferred_element_type=jnp.float32,
    )
    hot_gates = hot_parts[:, :hot_width]
    hot_ups = hot_parts[:, hot_width:]
    cold_gates = jnp.dot(arrived, cold_gate, preferred_element_type=jnp.float32)
    cold_ups = jnp.dot(arrived, cold_up, preferred_element_type=jnp.float32)
    hot_gates, hot_ups, cold_gates, cold_ups = lax.psum(
        (hot_gates, hot_ups, cold_gates, cold_ups), "hot"
    )
    hot_hidden = gated_hidden(hot_gates, hot_ups, hot_bits)
    cold_hidden = gated_hidden(cold_gates, cold_ups, arrived_bits)
    cold_out = jnp.dot(cold_hidden, cold_down, preferred_element_type=jnp.float32)
    returned = lax.all_to_all(
        cold_out.reshape(groups, slot_count, feature_cols),
        "cold",
        split_axis=0,
        concat_axis=0,
        tiled=True,
    )
    cold_mine = jnp.einsum(
        "gst,gsd->td", chosen.astype(jnp.float32), returned, precision=lax.Precision.HIGHEST
    )
    partial_value = jnp.dot(hot_hidden, hot_down, preferred_element_type=jnp.float32)
    combined = lax.psum_scatter(partial_value, "cold", scatter_dimension=0, tiled=True)
    combined = combined + cold_mine
    return combined.astype(jnp.bfloat16)


def solution(mesh):
    return jax.shard_map(
        body,
        mesh=mesh,
        in_specs=(
            P("cold", "hot"),
            P("hot", "cold"),
            P("hot", "cold"),
            P("cold", "hot"),
            P("hot", "cold"),
            P("hot", "cold"),
            P("cold", "hot"),
            P(),
            P(),
            P(),
        ),
        out_specs=P("cold", "hot"),
        check_vma=False,
    )
```

profile of v0, /device:TPU:0, one launch (start us, length us, event | category | flops | bytes accessed | tf_op | source)
XLA Modules:
  0.0 127.6 jit_solution(8542008087373703316)
XLA Ops:
  6.5 0.8 compare_select_fusion.2
  7.3 0.8 compare_and_fusion.1
  8.2 1.3 %gather_fusion = s32[48,128]{1,0:T(8,128)S(1)} fusion(s32[128,56]{0,1:T(8,128)} %param.19, s32[1024]{0:T(1024)S(1)} %pad_clamp_fusion.1), kind=kCustom, calls=%fused_computation | custom fusion | bytes 49344 | tf_op jit(solution)/shard_map/jit(_take)/gather | solution.py:34
  9.5 0.1 broadcast_in_dim.67
  9.6 0.1 select_reduce_fusion
  9.8 0.1 copy.21
  9.9 0.7 reduce-window_subtract_fusion
  10.7 1.7 %convolution_convert_fusion = bf16[8,8,2048]{2,1,0:T(8,128)(2,1)} fusion(bf16[16,2048]{1,0:T(8,128)(2,1)} %param.10, s32[8,16]{1,0:T(8,128)S(1)} %bitcast.57, pred[8,16]{1,0:T(8,128)(4,1)S(1)} %bitcast.59), kind=kOutput, calls=%fused_computation.4 | convolution fusion | flops 4327424 | bytes 328320 | tf_op jit(solution)/shard_map/gst,td->gsd/dot_general | solution.py:43
  12.4 5.2 %all-to-all-start = ((bf16[8,8,2048]{2,1,0:T(8,128)(2,1)}), bf16[8,8,2048]{2,1,0:T(8,128)(2,1)S(1)}, u32[]{:S(2)}, u32[]{:S(2)}) async-start(bf16[8,8,2048]{2,1,0:T(8,128)(2,1)} %convolution_convert_fusion), calls=%async_computation.1 | async-start | bytes 524288 | tf_op jit(solution)/shard_map/all_to_all | solution.py:46
  17.7 11.2 %all_gather.3 = bf16[128,2048]{1,0:T(8,128)(2,1)S(1)} all-gather(bf16[16,2048]{1,0:T(8,128)(2,1)} %param.10), channel_id=1, replica_groups=mesh['hot'=4,'cold'=8] {'cold'}, dimensions={0}, use_global_device_ids=true | all-gather | bytes 589824 | tf_op jit(solution)/shard_map/all_gather | solution.py:64
  28.9 1.2 dynamic_slice.20
  32.1 2.3 %convolution_bitcast_fusion.2 = f32[128,256]{0,1:T(8,128)} fusion(bf16[128,2048]{1,0:T(8,128)(2,1)S(1)} %all_gather.3, bf16[2048,128]{1,0:T(8,128)(2,1)} %param.12, bf16[2048,128]{1,0:T(8,128)(2,1)} %param.11), kind=kOutput, calls=%fused_computation.8 | convolution fusion | flops 136314880 | bytes 1703936 | tf_op jit(solution)/shard_map/dot_general | solution.py:63
  34.5 1.5 %fusion.31 = (f32[128,128]{0,1:T(8,128)}, f32[128,128]{0,1:T(8,128)}) fusion(f32[128,256]{0,1:T(8,128)} %convolution_bitcast_fusion.2), kind=kLoop, calls=%fused_computation.57 | loop fusion | bytes 262144 | tf_op jit(solution)/shard_map/slice | solution.py:68
  36.0 3.3 %fusion.5 = f32[64,768]{1,0:T(8,128)} fusion(bf16[2048,768]{1,0:T(8,128)(2,1)} %param.15, bf16[8,8,2048]{2,1,0:T(8,128)(2,1)S(1)} %all-to-all-done), kind=kOutput, calls=%fused_computation.13 | convolution fusion | flops 201326592 | bytes 3604480 | tf_op jit(solution)/shard_map/dot_general | solution.py:71
  39.4 1.3 %fusion.7 = f32[64,768]{1,0:T(8,128)} fusion(bf16[2048,768]{1,0:T(8,128)(2,1)S(1)} %copy-done.1, bf16[8,8,2048]{2,1,0:T(8,128)(2,1)S(1)} %all-to-all-done), kind=kOutput, calls=%fused_computation.15 | convolution fusion | flops 201326592 | bytes 3604480 | tf_op jit(solution)/shard_map/dot_general | solution.py:70
  40.7 0.7 fusion.24
  41.6 38.2 %all-reduce.4.cloned.1.call-done = (f32[128,128]{0,1:T(8,128)}, f32[128,128]{0,1:T(8,128)}, f32[64,768]{1,0:T(8,128)}, f32[64,768]{1,0:T(8,128)}) async-done(((f32[128,128]{0,1:T(8,128)}, f32[128,128]{0,1:T(8,128)}, f32[64,768]{1,0:T(8,128)}, f32[64,768]{1,0:T(8,128)}), (f32[128,128]{0,1:T(8,128)}, f32[128,128]{0,1:T(8,128)}, f32[64,768]{1,0:T(8,128)}, f32[64,768]{1,0:T(8,128)})) %all-reduce.4.cloned.1.call-update) | async-done | bytes 524304 | tf_op jit(solution)/shard_map/psum | solution.py:72
  79.8 2.5 %fusion.13 = f32[128,2048]{1,0:T(8,128)} fusion(bf16[128,2048]{1,0:T(8,128)(2,1)} %param.13, f32[128,128]{0,1:T(8,128)} %get-tuple-element.16, f32[128,128]{0,1:T(8,128)} %get-tuple-element.17, f32[128]{0:T(128)S(1)} %fusion.24), kind=kOutput, calls=%fused_computation.22 | convolution fusion | flops 67223552 | bytes 1704448 | tf_op jit(solution)/shard_map/dot_general | solution.py:88
  82.3 0.5 iota_multiply_fusion
  82.9 0.1 copy.27
  83.0 0.1 gt.38
  83.1 0.7 add.92
  83.8 0.1 add.93
  83.9 0.1 copy.24
  84.0 0.1 squeeze.11
  84.1 1.0 scatter_custom_fusion
  85.1 0.6 gather_fusion.1
  85.8 0.1 broadcast_in_dim.78
  85.9 1.6 %convolution_bitcast_fusion = f32[8,8,2048]{2,1,0:T(8,128)S(1)} fusion(bf16[768,2048]{1,0:T(8,128)(2,1)S(1)} %copy-done, f32[8,8,6,128]{3,2,1,0:T(8,128)S(1)} %bitcast.54, f32[64,768]{1,0:T(8,128)S(1)} %copy-done.2, f32[64,768]{1,0:T(8,128)} %get-tuple-element.19), kind=kOutput, calls=%fused_computation.3 | convolution fusion | flops 201670656 | bytes 4259840 | tf_op jit(solution)/shard_map/dot_general | solution.py:77
  87.5 13.1 %all_to_all.10 = f32[8,8,2048]{2,1,0:T(8,128)} all-to-all(f32[8,8,2048]{2,1,0:T(8,128)S(1)} %convolution_bitcast_fusion), channel_id=1, replica_groups=mesh['hot'=4,'cold'=8] {'cold'}, dimensions={0} | all-to-all | bytes 1048576 | tf_op jit(solution)/shard_map/all_to_all | solution.py:78
  100.6 18.2 %reduce-scatter.2.cloned.1.call-done = f32[16,2048]{1,0:T(8,128)} async-done(((f32[128,2048]{1,0:T(8,128)}), f32[16,2048]{1,0:T(8,128)}) %reduce-scatter.2.cloned.1.call-update) | async-done | bytes 131088 | tf_op jit(solution)/shard_map/reduce_scatter | solution.py:89
  118.8 2.0 %fusion.1 = bf16[16,2048]{1,0:T(8,128)(2,1)} fusion(f32[16,2048]{1,0:T(8,128)} %reduce-scatter.2.cloned.1.call-done, f32[8,8,2048]{2,1,0:T(8,128)} %all_to_all.10, s32[8,16]{1,0:T(8,128)S(1)} %bitcast.58, pred[8,16]{1,0:T(8,128)(4,1)S(1)} %bitcast.60), kind=kOutput, calls=%fused_computation.7 | convolution fusion | flops 25233408 | bytes 721536 | tf_op jit(solution)/shard_map/gst,gsd->td/dot_general | solution.py:85
  (28 shorter events, 0.7 us)
Async XLA Ops:
  6.5 79.4 %copy-start = (bf16[768,2048]{1,0:T(8,128)(2,1)S(1)}, bf16[768,2048]{1,0:T(8,128)(2,1)}, u32[]{:S(2)}) copy-start(bf16[768,2048]{1,0:T(8,128)(2,1)} %param.16) | copy-start | bytes 9437188
  12.4 23.6 %all-to-all-start = ((bf16[8,8,2048]{2,1,0:T(8,128)(2,1)}), bf16[8,8,2048]{2,1,0:T(8,128)(2,1)S(1)}, u32[]{:S(2)}, u32[]{:S(2)}) async-start(bf16[8,8,2048]{2,1,0:T(8,128)(2,1)} %convolution_convert_fusion), calls=%async_computation.1 | async-start | bytes 524288 | tf_op jit(solution)/shard_map/all_to_all | solution.py:46
  17.6 62.2 %all-reduce.4.cloned.1.call-start = ((), (), s32[]{:S(2)}) async-start(), calls=%async_computation.4 | async-start | bytes 1048576 | tf_op jit(solution)/shard_map/psum | solution.py:72
  36.0 3.3 %copy-start.1 = (bf16[2048,768]{1,0:T(8,128)(2,1)S(1)}, bf16[2048,768]{1,0:T(8,128)(2,1)}, u32[]{:S(2)}) copy-start(bf16[2048,768]{1,0:T(8,128)(2,1)} %param.14) | copy-start | bytes 9437188
  40.7 78.1 %reduce-scatter.2.cloned.1.call-start = ((), (), s32[]{:S(2)}) async-start(), calls=%async_computation.3 | async-start | bytes 1179648 | tf_op jit(solution)/shard_map/reduce_scatter | solution.py:89
  79.8 6.1 %copy-start.2 = (f32[64,768]{1,0:T(8,128)S(1)}, f32[64,768]{1,0:T(8,128)}, u32[]{:S(2)}) copy-start(f32[64,768]{1,0:T(8,128)} %get-tuple-element.18) | copy-start | bytes 589828
Sparse Core Ops, SparseCore 0:
  40.8 38.9 all-reduce.3
  83.0 35.7 reduce-scatter.1
where the time goes:
time: 128 us
  waiting for transfers between devices  56.4 us (44%)
  blocking collectives  24.3 us (19%)
  between operations  15.5 us (12%)
  matrix products  14.8 us (12%)
  local copies, waits for them, and re-layouts  7.53 us (6%)
  starting transfers between devices  5.28 us (4%)
  other arithmetic  3.81 us (3%)
    psum x1, waiting for transfers between devices, body(): lax.psum((hot_gates, hot_ups, cold_gates, cold_ups), 'hot')  38.2 us
    reduce_scatter x1, waiting for transfers between devices, body(): lax.psum_scatter(partial_value, 'cold', scatter_dimension=0, tiled=True)  18.2 us
    all_to_all x1, blocking collectives, body(): lax.all_to_all(cold_out.reshape(groups, slot_count, feature_cols), 'cold'...  13.1 us
    all_gather x1, blocking collectives, body(): lax.all_gather(tokens, 'cold', axis=0, tiled=True)  11.2 us
    all_to_all x1, starting transfers between devices, body(): lax.all_to_all(outgoing, 'cold', split_axis=0, concat_axis=0, tiled=True)  5.2 us
    dot_general x1, matrix products, body(): cold_ups = jnp.dot(arrived, cold_up, preferred_element_type=jnp.float32)  3.34 us
  transfers between devices with their start and end apart: 3, of which 2 were waited for; matrix products, arithmetic and copies ran while one was open for 9% of the time, Pallas kernels for 0%

commit v1 on v0

v1 whole, which is shorter than its diff:
```python
import functools

import jax
import jax.numpy as jnp
from jax import lax
from jax.experimental import pallas as pl
from jax.experimental.pallas import tpu as pltpu
from jax.sharding import PartitionSpec as P

BLOCK = 128
CHUNK = 256
OUT_CHUNK = 512
MESH = pl.DeviceIdType.MESH
NT = (((1,), (1,)), ((), ()))
SUM_TYPE = jnp.float32
OUT_TYPE = jnp.bfloat16


def dot(a, b):
    return jnp.dot(a, b, preferred_element_type=jnp.float32)


def dot_nt(a, b):
    return lax.dot_general(a, b, NT, preferred_element_type=jnp.float32)


def zero_one(condition):
    return jnp.where(condition, 1.0, 0.0).astype(jnp.bfloat16)


def hidden_of(sums, bits, first_slot):
    width = sums.shape[1] // 2
    gate, up = sums[:, :width], sums[:, width:]
    value = gate / (1.0 + jnp.exp(-gate)) * up
    pieces = [
        value[:, j * BLOCK:(j + 1) * BLOCK] * bits[:, first_slot + j:first_slot + j + 1]
        for j in range(width // BLOCK)
    ]
    return jnp.concatenate(pieces, axis=1).astype(jnp.bfloat16)


def kernel(
    n_hot, n_cold,
    tok_in, hg_in, hu_in, hd_in, cg_in, cu_in, cd_in, hid_in, cid_in, mask_in,
    out_ref,
    tok_all, w_hot, w_cold, w_down, hot_ids, cold_ids, mask,
    picked, bits_hot, bits_cold, spread,
    part_hot, part_cold, send_hot, send_cold, got_hot, got_cold,
    own_hot, own_cold, full, outs, pair_in, mine, ready, final_in,
    load_sem, tok_sem, tok_send, tok_recv, fwd_send, fwd_recv,
    rs_send, rs_recv, hg_send, hg_recv, pr_send, pr_recv, fin_send, fin_recv,
):
    me_hot, me_cold = lax.axis_index("hot"), lax.axis_index("cold")
    pairs = n_cold // 2
    my_pair, my_side = me_cold // 2, me_cold % 2
    other = my_pair * 2 + (1 - my_side)
    rows = tok_in.shape[0]
    tokens = tok_all.shape[0]
    hot_width = hg_in.shape[1]
    hot_slots = hot_width // BLOCK
    cold_width = cg_in.shape[1]
    cold_slots = cold_width // BLOCK
    chunks = cold_width // CHUNK
    slot_count = rows // 2
    picks = n_cold * slot_count
    hot_rows, cold_rows = tokens // n_hot, picks // n_hot
    cols = tok_in.shape[1]
    out_chunks = cols // OUT_CHUNK

    own_slot = tok_all.at[pl.ds(pl.multiple_of(me_cold * rows, rows), rows)]
    tok_load = pltpu.make_async_copy(tok_in, own_slot, tok_sem)
    tok_load.start()
    loads = []

    def load(src, dst):
        copy = pltpu.make_async_copy(src, dst, load_sem.at[len(loads)])
        copy.start()
        loads.append(copy)

    load(hid_in, hot_ids)
    load(cid_in, cold_ids)
    load(mask_in, mask)
    load(hg_in, w_hot.at[:, pl.ds(0, hot_width)])
    load(hu_in, w_hot.at[:, pl.ds(hot_width, hot_width)])
    for k in range(chunks):
        load(cg_in.at[:, pl.ds(k * CHUNK, CHUNK)], w_cold.at[k, :, pl.ds(0, CHUNK)])
        load(cu_in.at[:, pl.ds(k * CHUNK, CHUNK)], w_cold.at[k, :, pl.ds(CHUNK, CHUNK)])
    load(hd_in, w_down.at[pl.ds(0, hot_width)])
    load(cd_in, w_down.at[pl.ds(hot_width, cold_width)])

    barrier = pltpu.get_barrier_semaphore()
    hot_peers = [lax.rem(me_hot + k, n_hot) for k in range(1, n_hot)]
    pair_peers = [lax.rem(my_pair + k, pairs) for k in range(1, pairs)]
    for peer in hot_peers:
        pl.semaphore_signal(barrier, inc=1, device_id={"hot": peer}, device_id_type=MESH)
    for peer in pair_peers:
        pl.semaphore_signal(
            barrier, inc=1, device_id={"cold": peer * 2 + my_side}, device_id_type=MESH
        )
    pl.semaphore_signal(barrier, inc=1, device_id={"cold": other}, device_id_type=MESH)
    pl.semaphore_wait(barrier, n_hot - 1 + pairs - 1 + 1)

    sent = []

    def send(src, dst, s_sem, r_sem, device):
        copy = pltpu.make_async_remote_copy(
            src_ref=src, dst_ref=dst, send_sem=s_sem, recv_sem=r_sem,
            device_id=device, device_id_type=MESH,
        )
        copy.start()
        sent.append(copy)

    def arrive(dst, s_sem, r_sem, device):
        pltpu.make_async_remote_copy(
            src_ref=dst, dst_ref=dst, send_sem=s_sem, recv_sem=r_sem,
            device_id=device, device_id_type=MESH,
        ).wait_recv()

    tok_load.wait()
    for k, peer in enumerate(pair_peers):
        send(own_slot, own_slot, tok_send.at[k], tok_recv.at[my_pair],
             {"cold": peer * 2 + my_side})
    send(own_slot, own_slot, fwd_send.at[0], fwd_recv.at[my_pair], {"cold": other})

    for copy in loads[:3]:
        copy.wait()
    slots_pad = bits_hot.shape[1]
    blocks = mask.shape[1]
    slot_at = lax.broadcasted_iota(jnp.int32, (slots_pad, blocks), 0)
    id_at = jnp.full((slots_pad, blocks), -1, jnp.int32)
    for j in range(hot_slots):
        id_at = jnp.where(slot_at == j, hot_ids[me_cold * hot_slots + j], id_at)
    for j in range(cold_slots):
        id_at = jnp.where(slot_at == hot_slots + j, cold_ids[me_cold * cold_slots + j], id_at)
    chosen = zero_one(lax.broadcasted_iota(jnp.int32, (slots_pad, blocks), 1) == id_at)
    mask_value = mask[...].astype(jnp.float32).astype(jnp.bfloat16)
    bits_t = dot_nt(chosen, mask_value)
    slot_row = lax.broadcasted_iota(jnp.int32, (slots_pad, tokens), 0)
    is_cold = (slot_row >= hot_slots) & (slot_row < hot_slots + cold_slots)
    hit = jnp.max(jnp.where(is_cold, bits_t, 0.0), axis=0, keepdims=True)

    def group_of(shape, dim):
        at = lax.broadcasted_iota(jnp.int32, shape, dim)
        total = jnp.zeros(shape, jnp.int32)
        for g in range(1, n_cold):
            total = total + jnp.where(at >= g * rows, 1, 0)
        return total

    group_row, group_col = group_of((1, tokens), 1), group_of((tokens, 1), 0)
    before = lax.broadcasted_iota(jnp.int32, (tokens, tokens), 0) < lax.broadcasted_iota(
        jnp.int32, (tokens, tokens), 1
    )
    before = zero_one(before & (group_row == group_col))
    rank = dot(jnp.broadcast_to(hit, (8, tokens)).astype(jnp.bfloat16), before)[0:1]
    target = jnp.where(hit > 0.5, group_row * slot_count + rank.astype(jnp.int32), -1)
    pick = zero_one(lax.broadcasted_iota(jnp.int32, (picks, tokens), 0) == target)
    eye = zero_one(
        lax.broadcasted_iota(jnp.int32, (tokens, tokens), 0)
        == lax.broadcasted_iota(jnp.int32, (tokens, tokens), 1)
    )
    spread[...] = dot_nt(eye, pick).astype(jnp.bfloat16)
    bits_cold[...] = dot_nt(pick, bits_t.astype(jnp.bfloat16))
    bits_hot[...] = dot_nt(mask_value, chosen)

    def slot_of(device):
        return tok_all.at[pl.ds(pl.multiple_of(device * rows, rows), rows)]

    for k in range(1, pairs):
        source = lax.rem(my_pair + pairs - k, pairs)
        slot = slot_of(source * 2 + my_side)
        arrive(slot, tok_send.at[k - 1], tok_recv.at[source], {"cold": source * 2 + my_side})
        send(slot, slot, fwd_send.at[k], fwd_recv.at[source], {"cold": other})
    for k in range(pairs):
        source = lax.rem(my_pair + pairs - k, pairs)
        arrive(slot_of(source * 2 + (1 - my_side)), fwd_send.at[k], fwd_recv.at[source],
               {"cold": other})

    def part(index, value, kept, outgoing, incoming, count):
        kept[...] = value
        if outgoing is not kept:
            outgoing[...] = value.astype(outgoing.dtype)
        for k, peer in enumerate(hot_peers):
            send(
                outgoing.at[pl.ds(pl.multiple_of(peer * count, count), count)],
                incoming.at[me_hot],
                rs_send.at[index, k], rs_recv.at[index, me_hot], {"hot": peer},
            )

    loads[3].wait()
    loads[4].wait()
    picked[...] = dot(pick, tok_all[...]).astype(jnp.bfloat16)
    for k in range(chunks):
        loads[5 + 2 * k].wait()
        loads[6 + 2 * k].wait()
        part(k, dot(picked[...], w_cold[k]), part_cold.at[k], send_cold.at[k],
             got_cold.at[k], cold_rows)
    part(chunks, dot(tok_all[...], w_hot[...]), part_hot, send_hot, got_hot, hot_rows)

    def finish(index, kept, incoming, count, bits, first_slot, held):
        own = pl.ds(pl.multiple_of(me_hot * count, count), count)
        total = kept[own]
        for k in range(1, n_hot):
            source = lax.rem(me_hot + n_hot - k, n_hot)
            arrive(incoming.at[source], rs_send.at[index, k - 1], rs_recv.at[index, source],
                   {"hot": source})
            total = total + incoming[source].astype(jnp.float32)
        held[own] = hidden_of(total, bits[own], first_slot)
        for k, peer in enumerate(hot_peers):
            send(held.at[own], held.at[own], hg_send.at[index, k], hg_recv.at[index, me_hot],
                 {"hot": peer})

    for k in range(chunks):
        finish(k, part_cold.at[k], got_cold.at[k], cold_rows, bits_cold,
               hot_slots + k * (CHUNK // BLOCK), own_cold.at[k])
    finish(chunks, part_hot, got_hot, hot_rows, bits_hot, 0, own_hot)

    def gathered(index, count, held):
        for k in range(1, n_hot):
            source = lax.rem(me_hot + n_hot - k, n_hot)
            arrive(held.at[pl.ds(pl.multiple_of(source * count, count), count)],
                   hg_send.at[index, k - 1], hg_recv.at[index, source], {"hot": source})

    for k in range(chunks):
        gathered(k, cold_rows, own_cold.at[k])
        full[:, hot_width + k * CHUNK:hot_width + (k + 1) * CHUNK] = dot(
            spread[...], own_cold[k]
        ).astype(jnp.bfloat16)
    gathered(chunks, hot_rows, own_hot)
    full[:, :hot_width] = own_hot[...]

    for copy in loads[5 + 2 * chunks:]:
        copy.wait()
    for c in range(out_chunks):
        at = pl.ds(c * OUT_CHUNK, OUT_CHUNK)
        value = dot(full[...], w_down[:, c * OUT_CHUNK:(c + 1) * OUT_CHUNK])
        outs[:, :, :, at] = value.reshape(pairs, 2, rows, OUT_CHUNK)
        send(outs.at[:, 1 - my_side, :, at], pair_in.at[:, :, at],
             pr_send.at[c], pr_recv.at[c], {"cold": other})
    for c in range(out_chunks):
        at = pl.ds(c * OUT_CHUNK, OUT_CHUNK)
        arrive(pair_in.at[:, :, at], pr_send.at[c], pr_recv.at[c], {"cold": other})
        value = outs[:, my_side, :, at] + pair_in[:, :, at]
        mine[:, :, at] = value
        ready[:, :, at] = value.astype(ready.dtype)
        for k, peer in enumerate(pair_peers):
            send(ready.at[peer, :, at], final_in.at[my_pair, :, at],
                 fin_send.at[c, k], fin_recv.at[c, my_pair], {"cold": peer * 2 + my_side})
    for c in range(out_chunks):
        at = pl.ds(c * OUT_CHUNK, OUT_CHUNK)
        total = mine[my_pair, :, at]
        for k in range(1, pairs):
            source = lax.rem(my_pair + pairs - k, pairs)
            arrive(final_in.at[source, :, at], fin_send.at[c, k - 1], fin_recv.at[c, source],
                   {"cold": source * 2 + my_side})
            total = total + final_in[source, :, at].astype(jnp.float32)
        out_ref[:, at] = total.astype(out_ref.dtype)
    for copy in sent:
        copy.wait_send()


def body(n_hot, n_cold, *args):
    (tokens, hot_gate, hot_up, hot_down, cold_gate, cold_up, cold_down,
     hot_ids, cold_ids, block_mask) = args
    rows, cols = tokens.shape
    total_rows = block_mask.shape[0]
    hot_width, cold_width = hot_gate.shape[1], cold_gate.shape[1]
    chunks = cold_width // CHUNK
    picks = n_cold * (rows // 2)
    pairs = n_cold // 2
    slots_pad = -(-((hot_width + cold_width) // BLOCK) // 8) * 8
    hot_rows, cold_rows = total_rows // n_hot, picks // n_hot
    out_chunks = cols // OUT_CHUNK
    bf16, f32, i32 = jnp.bfloat16, jnp.float32, jnp.int32
    vmem, dma = pltpu.VMEM, pltpu.SemaphoreType.DMA
    scratch = [
        vmem((total_rows, cols), bf16),
        vmem((cols, 2 * hot_width), bf16),
        vmem((chunks, cols, 2 * CHUNK), bf16),
        vmem((hot_width + cold_width, cols), bf16),
        pltpu.SMEM(hot_ids.shape, i32),
        pltpu.SMEM(cold_ids.shape, i32),
        vmem(block_mask.shape, i32),
        vmem((picks, cols), bf16),
        vmem((total_rows, slots_pad), f32),
        vmem((picks, slots_pad), f32),
        vmem((total_rows, picks), bf16),
        vmem((total_rows, 2 * hot_width), f32),
        vmem((chunks, picks, 2 * CHUNK), f32),
        vmem((total_rows, 2 * hot_width), SUM_TYPE),
        vmem((chunks, picks, 2 * CHUNK), SUM_TYPE),
        vmem((n_hot, hot_rows, 2 * hot_width), SUM_TYPE),
        vmem((chunks, n_hot, cold_rows, 2 * CHUNK), SUM_TYPE),
        vmem((total_rows, hot_width), bf16),
        vmem((chunks, picks, CHUNK), bf16),
        vmem((total_rows, hot_width + cold_width), bf16),
        vmem((pairs, 2, rows, cols), f32),
        vmem((pairs, rows, cols), f32),
        vmem((pairs, rows, cols), f32),
        vmem((pairs, rows, cols), OUT_TYPE),
        vmem((pairs, rows, cols), OUT_TYPE),
        dma((7 + 2 * chunks,)),
        dma,
        dma((pairs,)),
        dma((pairs,)),
        dma((pairs,)),
        dma((pairs,)),
        dma((chunks + 1, n_hot)),
        dma((chunks + 1, n_hot)),
        dma((chunks + 1, n_hot)),
        dma((chunks + 1, n_hot)),
        dma((out_chunks,)),
        dma((out_chunks,)),
        dma((out_chunks, pairs)),
        dma((out_chunks, pairs)),
    ]
    return pl.pallas_call(
        functools.partial(kernel, n_hot, n_cold),
        out_shape=jax.ShapeDtypeStruct((rows, cols), bf16),
        in_specs=[pl.BlockSpec(memory_space=pl.ANY)] * 10,
        out_specs=pl.BlockSpec(memory_space=pltpu.VMEM),
        scratch_shapes=scratch,
        compiler_params=pltpu.CompilerParams(
            collective_id=0, has_side_effects=True, vmem_limit_bytes=60 * 1024 * 1024
        ),
        name="decode_step",
    )(*args)


def solution(mesh):
    return jax.shard_map(
        functools.partial(body, mesh.shape["hot"], mesh.shape["cold"]),
        mesh=mesh,
        in_specs=(
            P("cold", "hot"),
            P("hot", "cold"),
            P("hot", "cold"),
            P("cold", "hot"),
            P("hot", "cold"),
            P("hot", "cold"),
            P("cold", "hot"),
            P(),
            P(),
            P(),
        ),
        out_specs=P("cold", "hot"),
        check_vma=False,
    )
```

time: 128 us -> 42.2 us (0.33)
  waiting for transfers between devices: 56.4 us -> 0 us
  Pallas kernels: 0 us -> 39 us
  blocking collectives: 24.3 us -> 0 us
  between operations: 15.5 us -> 0.01 us
  matrix products: 14.8 us -> 0 us
  starting transfers between devices: 5.28 us -> 0 us
  local copies, waits for them, and re-layouts: 7.53 us -> 2.95 us
  other arithmetic: 3.81 us -> 0 us
    pallas_call x0 -> x1, Pallas kernels: none -> 39 us  [body(): pl.pallas_call(functools.partial(kernel, n_hot, n_cold), out_shape=jax.Sh...]
    psum x1 -> x0, waiting for transfers between devices: 38.2 us -> none  [body(): lax.psum((hot_gates, hot_ups, cold_gates, cold_ups), 'hot')]
    reduce_scatter x1 -> x0, waiting for transfers between devices: 18.2 us -> none  [body(): lax.psum_scatter(partial_value, 'cold', scatter_dimension=0, tiled=True)]
    dot_general x7 -> x0, matrix products: 14.8 us -> none  [the longest x1 3.34 us: body(): cold_ups = jnp.dot(arrived, cold_up, preferred_element_type=jnp.float32)]
    all_to_all x1 -> x0, blocking collectives: 13.1 us -> none  [body(): lax.all_to_all(cold_out.reshape(groups, slot_count, feature_cols), 'cold'...]
    all_gather x1 -> x0, blocking collectives: 11.2 us -> none  [body(): lax.all_gather(tokens, 'cold', axis=0, tiled=True)]
    all_to_all x1 -> x0, starting transfers between devices: 5.2 us -> none  [body(): lax.all_to_all(outgoing, 'cold', split_axis=0, concat_axis=0, tiled=True)]
    unnamed x8 -> x2, local copies, waits for them, and re-layouts: 0.13 us -> 2.95 us
  transfers between devices with their start and end apart: 3 -> 0, of which waited for: 2 -> 0; matrix products, arithmetic and copies ran while one was open for 9% -> 0% of each run, Pallas kernels for 0% -> 0%
where the time goes in v1:
time: 42.2 us; the launch traced here: 42 us
  Pallas kernels  39 us (92%)
  local copies, waits for them, and re-layouts  2.95 us (7%)
    pallas_call x1, Pallas kernels, body(): pl.pallas_call(functools.partial(kernel, n_hot, n_cold), out_shape=jax.Sh...  39 us
    unnamed x2, local copies, waits for them, and re-layouts  2.95 us

profile of v1, /device:TPU:0, one launch (start us, length us, event | category | flops | bytes accessed | tf_op | source)
XLA Modules:
  0.0 42.0 jit_solution(16932057155810410447)
XLA Ops:
  0.0 1.5 %copy.11.mask_in = s32[128,56]{1,0:T(8,128)} copy(s32[128,56]{0,1:T(8,128)} %param.19) | data formatting | bytes 57344 | tf_op args[9]
  1.5 39.0 %decode_step.1 = bf16[16,2048]{1,0:T(8,128)(2,1)} custom-call(bf16[16,2048]{1,0:T(8,128)(2,1)} %tok_in.1, bf16[2048,128]{1,0:T(8,128)(2,1)} %hg_in.1, bf16[2048,128]{1,0:T(8,128)(2,1)} %hu_in.1, bf16[128,2048]{1,0:T(8,128)(2,1)} %hd_in.1, bf16[2048,768]{1,0:T(8,128)(2,1)} %cg_in.1, bf16[2048,768]{1,0:T(8,128)(2,1)} %cu_in.1, bf16[768,2048]{1,0:T(8,128)(2,1)} %cd_in.1, ...), custom_call_target="tpu_custom_call" | custom-call | tf_op jit(solution)/shard_map/decode_step/pallas_call | solution.py:316
  40.5 1.5 %copy.13 = bf16[16,2048]{1,0:T(8,128)(2,1)} copy(bf16[16,2048]{1,0:T(8,128)(2,1)} %decode_step.1) | data formatting | bytes 131072

commit v2 on v1

--- a/solution.py
+++ b/solution.py
@@ -12,7 +12,7 @@
 OUT_CHUNK = 512
 MESH = pl.DeviceIdType.MESH
 NT = (((1,), (1,)), ((), ()))
-SUM_TYPE = jnp.float32
+SUM_TYPE = jnp.bfloat16
 OUT_TYPE = jnp.bfloat16
 
 
@@ -125,7 +125,7 @@
     for copy in loads[:3]:
         copy.wait()
     slots_pad = bits_hot.shape[1]
-    blocks = mask.shape[1]
+    blocks = mask.shape[0]
     slot_at = lax.broadcasted_iota(jnp.int32, (slots_pad, blocks), 0)
     id_at = jnp.full((slots_pad, blocks), -1, jnp.int32)
     for j in range(hot_slots):
@@ -134,7 +134,7 @@
         id_at = jnp.where(slot_at == hot_slots + j, cold_ids[me_cold * cold_slots + j], id_at)
     chosen = zero_one(lax.broadcasted_iota(jnp.int32, (slots_pad, blocks), 1) == id_at)
     mask_value = mask[...].astype(jnp.float32).astype(jnp.bfloat16)
-    bits_t = dot_nt(chosen, mask_value)
+    bits_t = dot(chosen, mask_value)
     slot_row = lax.broadcasted_iota(jnp.int32, (slots_pad, tokens), 0)
     is_cold = (slot_row >= hot_slots) & (slot_row < hot_slots + cold_slots)
     hit = jnp.max(jnp.where(is_cold, bits_t, 0.0), axis=0, keepdims=True)
@@ -160,7 +160,7 @@
     )
     spread[...] = dot_nt(eye, pick).astype(jnp.bfloat16)
     bits_cold[...] = dot_nt(pick, bits_t.astype(jnp.bfloat16))
-    bits_hot[...] = dot_nt(mask_value, chosen)
+    bits_hot[...] = dot_nt(eye, bits_t.astype(jnp.bfloat16))
 
     def slot_of(device):
         return tok_all.at[pl.ds(pl.multiple_of(device * rows, rows), rows)]
@@ -279,7 +279,7 @@
         vmem((hot_width + cold_width, cols), bf16),
         pltpu.SMEM(hot_ids.shape, i32),
         pltpu.SMEM(cold_ids.shape, i32),
-        vmem(block_mask.shape, i32),
+        vmem(block_mask.shape[::-1], i32),
         vmem((picks, cols), bf16),
         vmem((total_rows, slots_pad), f32),
         vmem((picks, slots_pad), f32),
@@ -323,7 +323,7 @@
             collective_id=0, has_side_effects=True, vmem_limit_bytes=60 * 1024 * 1024
         ),
         name="decode_step",
-    )(*args)
+    )(*args[:-1], block_mask.T)
 
 
 def solution(mesh):

time: 42.2 us -> 34.4 us (0.82)
  Pallas kernels: 39 us -> 32.8 us
  local copies, waits for them, and re-layouts: 2.95 us -> 1.47 us
    pallas_call x1, Pallas kernels: 39 us -> 32.8 us  [body(): pl.pallas_call(functools.partial(kernel, n_hot, n_cold), out_shape=jax.Sh...]
    unnamed x2 -> x1, local copies, waits for them, and re-layouts: 2.95 us -> 1.47 us
where the time goes in v2:
time: 34.4 us; the launch traced here: 34.2 us
  Pallas kernels  32.8 us (95%)
  local copies, waits for them, and re-layouts  1.47 us (4%)
    pallas_call x1, Pallas kernels, body(): pl.pallas_call(functools.partial(kernel, n_hot, n_cold), out_shape=jax.Sh...  32.8 us
    unnamed x1, local copies, waits for them, and re-layouts  1.47 us

profile of v2, /device:TPU:0, one launch (start us, length us, event | category | flops | bytes accessed | tf_op | source)
XLA Modules:
  0.0 34.2 jit_solution(7528664630441843156)
XLA Ops:
  0.0 32.8 %decode_step.1 = bf16[16,2048]{1,0:T(8,128)(2,1)} custom-call(bf16[16,2048]{1,0:T(8,128)(2,1)} %tok_in.1, bf16[2048,128]{1,0:T(8,128)(2,1)} %hg_in.1, bf16[2048,128]{1,0:T(8,128)(2,1)} %hu_in.1, bf16[128,2048]{1,0:T(8,128)(2,1)} %hd_in.1, bf16[2048,768]{1,0:T(8,128)(2,1)} %cg_in.1, bf16[2048,768]{1,0:T(8,128)(2,1)} %cu_in.1, bf16[768,2048]{1,0:T(8,128)(2,1)} %cd_in.1, ...), custom_call_target="tpu_custom_call" | custom-call | tf_op jit(solution)/shard_map/decode_step/pallas_call | solution.py:316
  32.8 1.5 %copy.12 = bf16[16,2048]{1,0:T(8,128)(2,1)} copy(bf16[16,2048]{1,0:T(8,128)(2,1)} %decode_step.1) | data formatting | bytes 131072

commit v3 on v2

v3 whole, which is shorter than its diff:
```python
import functools

import jax
import jax.numpy as jnp
from jax import lax
from jax.experimental import pallas as pl
from jax.experimental.pallas import tpu as pltpu
from jax.sharding import PartitionSpec as P

BLOCK = 128
CHUNK = 384
OUT_CHUNK = 1024
MESH = pl.DeviceIdType.MESH
NT = (((1,), (1,)), ((), ()))
SUM_TYPE = jnp.bfloat16
OUT_TYPE = jnp.bfloat16


def dot(a, b):
    return jnp.dot(a, b, preferred_element_type=jnp.float32)


def dot_nt(a, b):
    return lax.dot_general(a, b, NT, preferred_element_type=jnp.float32)


def zero_one(condition):
    return jnp.where(condition, 1.0, 0.0).astype(jnp.bfloat16)


def hidden_of(sums, bits, first_slot):
    width = sums.shape[1] // 2
    gate, up = sums[:, :width], sums[:, width:]
    value = gate / (1.0 + jnp.exp(-gate)) * up
    pieces = [
        value[:, j * BLOCK:(j + 1) * BLOCK] * bits[:, first_slot + j:first_slot + j + 1]
        for j in range(width // BLOCK)
    ]
    return jnp.concatenate(pieces, axis=1).astype(jnp.bfloat16)


def kernel(
    n_hot, n_cold,
    tok_in, hg_in, hu_in, hd_in, cg_in, cu_in, cd_in, hid_in, cid_in, mask_in,
    out_ref,
    tok_all, w_hot, w_cold, w_down, hot_ids, cold_ids, mask,
    picks_of, picked, bits_hot, bits_cold, spread,
    part_hot, part_cold, send_hot, send_cold, got_hot, got_cold,
    own_hot, own_cold, full, outs, pair_in, mine, ready, final_in,
    load_sem, tok_sem, tok_send, tok_recv, fwd_send, fwd_recv,
    rs_send, rs_recv, hg_send, hg_recv, pr_send, pr_recv, fin_send, fin_recv,
):
    me_hot, me_cold = lax.axis_index("hot"), lax.axis_index("cold")
    pairs = n_cold // 2
    span = pairs // 2
    my_pair, my_side = me_cold // 2, me_cold % 2
    my_half, my_place = my_pair // span, my_pair % span
    halves = (my_half, 1 - my_half)
    other = my_pair * 2 + (1 - my_side)
    rows = tok_in.shape[0]
    stage_tokens = tok_all.shape[0] // 2
    hot_width = hg_in.shape[1]
    hot_slots = hot_width // BLOCK
    cold_width = cg_in.shape[1]
    cold_slots = cold_width // BLOCK
    chunks = cold_width // CHUNK
    slot_count = rows // 2
    stage_picks = (n_cold // 2) * slot_count
    hot_rows, cold_rows = stage_tokens // n_hot, stage_picks // n_hot
    cols = tok_in.shape[1]
    out_chunks = cols // OUT_CHUNK

    own_slot = tok_all.at[pl.ds(pl.multiple_of(me_cold * rows, rows), rows)]
    tok_load = pltpu.make_async_copy(tok_in, own_slot, tok_sem)
    tok_load.start()
    loads = []

    def load(src, dst):
        copy = pltpu.make_async_copy(src, dst, load_sem.at[len(loads)])
        copy.start()
        loads.append(copy)

    def load_cold(k):
        load(cg_in.at[:, pl.ds(k * CHUNK, CHUNK)], w_cold.at[k, :, pl.ds(0, CHUNK)])
        load(cu_in.at[:, pl.ds(k * CHUNK, CHUNK)], w_cold.at[k, :, pl.ds(CHUNK, CHUNK)])

    load(hid_in, hot_ids)
    load(cid_in, cold_ids)
    load(mask_in, mask)
    load_cold(0)

    barrier = pltpu.get_barrier_semaphore()
    hot_peers = [lax.rem(me_hot + k, n_hot) for k in range(1, n_hot)]
    near_places = [lax.rem(my_place + k, span) for k in range(1, span)]
    far_places = [lax.rem(my_place + k, span) for k in range(span)]
    places = (near_places, far_places)
    pair_peers = [my_half * span + at for at in near_places]
    pair_peers += [(1 - my_half) * span + at for at in far_places]
    sources = [my_half * span + lax.rem(my_place + span - k, span) for k in range(1, span)]
    sources += [(1 - my_half) * span + lax.rem(my_place + span - k, span) for k in range(span)]
    for peer in hot_peers:
        pl.semaphore_signal(barrier, inc=1, device_id={"hot": peer}, device_id_type=MESH)
    for peer in pair_peers:
        pl.semaphore_signal(
            barrier, inc=1, device_id={"cold": peer * 2 + my_side}, device_id_type=MESH
        )
    pl.semaphore_signal(barrier, inc=1, device_id={"cold": other}, device_id_type=MESH)
    pl.semaphore_wait(barrier, n_hot - 1 + pairs - 1 + 1)

    sent = []

    def send(src, dst, s_sem, r_sem, device):
        copy = pltpu.make_async_remote_copy(
            src_ref=src, dst_ref=dst, send_sem=s_sem, recv_sem=r_sem,
            device_id=device, device_id_type=MESH,
        )
        copy.start()
        sent.append(copy)

    def arrive(dst, s_sem, r_sem, device):
        pltpu.make_async_remote_copy(
            src_ref=dst, dst_ref=dst, send_sem=s_sem, recv_sem=r_sem,
            device_id=device, device_id_type=MESH,
        ).wait_recv()

    tok_load.wait()
    for k, peer in enumerate(pair_peers):
        send(own_slot, own_slot, tok_send.at[k], tok_recv.at[my_pair],
             {"cold": peer * 2 + my_side})
    send(own_slot, own_slot, fwd_send.at[0], fwd_recv.at[my_pair], {"cold": other})
    for k in range(1, chunks):
        load_cold(k)
    load(hg_in, w_hot.at[:, pl.ds(0, hot_width)])
    load(hu_in, w_hot.at[:, pl.ds(hot_width, hot_width)])
    load(hd_in, w_down.at[pl.ds(0, hot_width)])
    load(cd_in, w_down.at[pl.ds(hot_width, cold_width)])

    for copy in loads[:3]:
        copy.wait()
    slots_pad = bits_hot.shape[-1]
    blocks = mask.shape[0]
    slot_at = lax.broadcasted_iota(jnp.int32, (slots_pad, blocks), 0)
    id_at = jnp.full((slots_pad, blocks), -1, jnp.int32)
    for j in range(hot_slots):
        id_at = jnp.where(slot_at == j, hot_ids[me_cold * hot_slots + j], id_at)
    for j in range(cold_slots):
        id_at = jnp.where(slot_at == hot_slots + j, cold_ids[me_cold * cold_slots + j], id_at)
    chosen = zero_one(lax.broadcasted_iota(jnp.int32, (slots_pad, blocks), 1) == id_at)
    mask_value = mask[...].astype(jnp.float32).astype(jnp.bfloat16)
    all_bits = dot(chosen, mask_value)

    def group_of(shape, dim):
        at = lax.broadcasted_iota(jnp.int32, shape, dim)
        total = jnp.zeros(shape, jnp.int32)
        for g in range(1, n_cold // 2):
            total = total + jnp.where(at >= g * rows, 1, 0)
        return total

    square = (stage_tokens, stage_tokens)
    row_at = lax.broadcasted_iota(jnp.int32, square, 0)
    col_at = lax.broadcasted_iota(jnp.int32, square, 1)
    group_row, group_col = group_of((1, stage_tokens), 1), group_of((stage_tokens, 1), 0)
    before = zero_one((row_at < col_at) & (group_row == group_col))
    eye = zero_one(row_at == col_at)
    slot_row = lax.broadcasted_iota(jnp.int32, (slots_pad, stage_tokens), 0)
    is_cold = (slot_row >= hot_slots) & (slot_row < hot_slots + cold_slots)
    pick_at = lax.broadcasted_iota(jnp.int32, (stage_picks, stage_tokens), 0)
    for s in range(2):
        bits_t = jnp.where(
            halves[s] == 0, all_bits[:, :stage_tokens], all_bits[:, stage_tokens:]
        )
        hit = jnp.max(jnp.where(is_cold, bits_t, 0.0), axis=0, keepdims=True)
        rank = dot(jnp.broadcast_to(hit, (8, stage_tokens)).astype(jnp.bfloat16), before)[0:1]
        target = jnp.where(hit > 0.5, group_row * slot_count + rank.astype(jnp.int32), -1)
        pick = zero_one(pick_at == target)
        picks_of[s] = pick
        spread[s] = dot_nt(eye, pick).astype(jnp.bfloat16)
        narrow = bits_t.astype(jnp.bfloat16)
        bits_cold[s] = dot_nt(pick, narrow).reshape(n_hot, cold_rows, slots_pad)
        bits_hot[s] = dot_nt(eye, narrow).reshape(n_hot, hot_rows, slots_pad)

    def slot_of(device):
        return tok_all.at[pl.ds(pl.multiple_of(device * rows, rows), rows)]

    def forward(which):
        for k in which:
            source = sources[k]
            slot = slot_of(source * 2 + my_side)
            arrive(slot, tok_send.at[k], tok_recv.at[source], {"cold": source * 2 + my_side})
            send(slot, slot, fwd_send.at[k + 1], fwd_recv.at[source], {"cold": other})

    def forwarded(which):
        for k in which:
            source = my_pair if k < 0 else sources[k]
            arrive(slot_of(source * 2 + (1 - my_side)), fwd_send.at[k + 1], fwd_recv.at[source],
                   {"cold": other})

    def part(s, index, value, kept, outgoing, incoming):
        value = value.reshape(kept.shape)
        kept[...] = value
        outgoing[...] = value.astype(outgoing.dtype)
        for k, peer in enumerate(hot_peers):
            send(outgoing.at[peer], incoming.at[me_hot],
                 rs_send.at[s, index, k], rs_recv.at[s, index, me_hot], {"hot": peer})

    def parts(s):
        here = tok_all.at[pl.ds(pl.multiple_of(halves[s] * stage_tokens, stage_tokens), stage_tokens)]
        picked[s] = dot(picks_of[s], here[...]).astype(jnp.bfloat16)
        for k in range(chunks):
            if s == 0:
                loads[3 + 2 * k].wait()
                loads[4 + 2 * k].wait()
            part(s, k, dot(picked[s], w_cold[k]), part_cold.at[s, k], send_cold.at[s, k],
                 got_cold.at[s, k])
        if s == 0:
            forward(range(span - 1, pairs - 1))
            loads[3 + 2 * chunks].wait()
            loads[4 + 2 * chunks].wait()
        part(s, chunks, dot(here[...], w_hot[...]), part_hot.at[s], send_hot.at[s], got_hot.at[s])

    forward(range(span - 1))
    forwarded(range(-1, span - 1))
    parts(0)
    forwarded(range(span - 1, pairs - 1))
    parts(1)

    def finish(s, index, kept, incoming, bits, first_slot, held):
        total = kept[me_hot]
        for k in range(1, n_hot):
            source = lax.rem(me_hot + n_hot - k, n_hot)
            arrive(incoming.at[source], rs_send.at[s, index, k - 1],
                   rs_recv.at[s, index, source], {"hot": source})
            total = total + incoming[source].astype(jnp.float32)
        held[me_hot] = hidden_of(total, bits[me_hot], first_slot)
        for k, peer in enumerate(hot_peers):
            send(held.at[me_hot], held.at[me_hot], hg_send.at[s, index, k],
                 hg_recv.at[s, index, me_hot], {"hot": peer})

    for s in range(2):
        for k in range(chunks):
            finish(s, k, part_cold.at[s, k], got_cold.at[s, k], bits_cold.at[s],
                   hot_slots + k * (CHUNK // BLOCK), own_cold.at[s, k])
        finish(s, chunks, part_hot.at[s], got_hot.at[s], bits_hot.at[s], 0, own_hot.at[s])

    def gathered(s, index, held):
        for k in range(1, n_hot):
            source = lax.rem(me_hot + n_hot - k, n_hot)
            arrive(held.at[source], hg_send.at[s, index, k - 1], hg_recv.at[s, index, source],
                   {"hot": source})
        value = held[...].astype(jnp.float32)
        return value.reshape(value.shape[0] * value.shape[1], value.shape[2]).astype(jnp.bfloat16)

    def down(s):
        for k in range(chunks):
            full[s, :, hot_width + k * CHUNK:hot_width + (k + 1) * CHUNK] = dot(
                spread[s], gathered(s, k, own_cold.at[s, k])
            ).astype(jnp.bfloat16)
        full[s, :, :hot_width] = gathered(s, chunks, own_hot.at[s])
        if s == 0:
            for copy in loads[5 + 2 * chunks:]:
                copy.wait()
        for c in range(out_chunks):
            at = pl.ds(c * OUT_CHUNK, OUT_CHUNK)
            value = dot(full[s], w_down[:, c * OUT_CHUNK:(c + 1) * OUT_CHUNK])
            outs[s, :, :, :, at] = value.reshape(span, 2, rows, OUT_CHUNK)
            send(outs.at[s, :, 1 - my_side, :, at], pair_in.at[s, :, :, at],
                 pr_send.at[s, c], pr_recv.at[s, c], {"cold": other})

    def combine(s):
        for c in range(out_chunks):
            at = pl.ds(c * OUT_CHUNK, OUT_CHUNK)
            arrive(pair_in.at[s, :, :, at], pr_send.at[s, c], pr_recv.at[s, c], {"cold": other})
            value = outs[s, :, my_side, :, at] + pair_in[s, :, :, at]
            if s == 0:
                mine[:, :, at] = value
            ready[s, :, :, at] = value.astype(ready.dtype)
            for k, place in enumerate(places[s]):
                send(ready.at[s, place, :, at], final_in.at[my_pair, :, at],
                     fin_send.at[s, c, k], fin_recv.at[c, my_pair],
                     {"cold": (halves[s] * span + place) * 2 + my_side})

    for s in range(2):
        down(s)
        combine(s)
    for c in range(out_chunks):
        at = pl.ds(c * OUT_CHUNK, OUT_CHUNK)
        total = mine[my_place, :, at]
        for source in sources:
            arrive(final_in.at[source, :, at], fin_send.at[0, c, 0], fin_recv.at[c, source],
                   {"cold": source * 2 + my_side})
            total = total + final_in[source, :, at].astype(jnp.float32)
        out_ref[:, at] = total.astype(out_ref.dtype)
    for copy in sent:
        copy.wait_send()


def body(n_hot, n_cold, *args):
    (tokens, hot_gate, hot_up, hot_down, cold_gate, cold_up, cold_down,
     hot_ids, cold_ids, block_mask) = args
    rows, cols = tokens.shape
    total_rows = block_mask.shape[0]
    hot_width, cold_width = hot_gate.shape[1], cold_gate.shape[1]
    chunks = cold_width // CHUNK
    pairs = n_cold // 2
    span = pairs // 2
    stage_tokens, stage_picks = total_rows // 2, span * 2 * (rows // 2)
    slots_pad = -(-((hot_width + cold_width) // BLOCK) // 8) * 8
    hot_rows, cold_rows = stage_tokens // n_hot, stage_picks // n_hot
    out_chunks = cols // OUT_CHUNK
    bf16, f32, i32 = jnp.bfloat16, jnp.float32, jnp.int32
    vmem, dma = pltpu.VMEM, pltpu.SemaphoreType.DMA
    scratch = [
        vmem((total_rows, cols), bf16),
        vmem((cols, 2 * hot_width), bf16),
        vmem((chunks, cols, 2 * CHUNK), bf16),
        vmem((hot_width + cold_width, cols), bf16),
        pltpu.SMEM(hot_ids.shape, i32),
        pltpu.SMEM(cold_ids.shape, i32),
        vmem(block_mask.shape[::-1], i32),
        vmem((2, stage_picks, stage_tokens), bf16),
        vmem((2, stage_picks, cols), bf16),
        vmem((2, n_hot, hot_rows, slots_pad), f32),
        vmem((2, n_hot, cold_rows, slots_pad), f32),
        vmem((2, stage_tokens, stage_picks), bf16),
        vmem((2, n_hot, hot_rows, 2 * hot_width), f32),
        vmem((2, chunks, n_hot, cold_rows, 2 * CHUNK), f32),
        vmem((2, n_hot, hot_rows, 2 * hot_width), SUM_TYPE),
        vmem((2, chunks, n_hot, cold_rows, 2 * CHUNK), SUM_TYPE),
        vmem((2, n_hot, hot_rows, 2 * hot_width), SUM_TYPE),
        vmem((2, chunks, n_hot, cold_rows, 2 * CHUNK), SUM_TYPE),
        vmem((2, n_hot, hot_rows, hot_width), bf16),
        vmem((2, chunks, n_hot, cold_rows, CHUNK), bf16),
        vmem((2, stage_tokens, hot_width + cold_width), bf16),
        vmem((2, span, 2, rows, cols), f32),
        vmem((2, span, rows, cols), f32),
        vmem((span, rows, cols), f32),
        vmem((2, span, rows, cols), OUT_TYPE),
        vmem((pairs, rows, cols), OUT_TYPE),
        dma((7 + 2 * chunks,)),
        dma,
        dma((pairs,)),
        dma((pairs,)),
        dma((pairs,)),
        dma((pairs,)),
        dma((2, chunks + 1, n_hot)),
        dma((2, chunks + 1, n_hot)),
        dma((2, chunks + 1, n_hot)),
        dma((2, chunks + 1, n_hot)),
        dma((2, out_chunks)),
        dma((2, out_chunks)),
        dma((2, out_chunks, span)),
        dma((out_chunks, pairs)),
    ]
    return pl.pallas_call(
        functools.partial(kernel, n_hot, n_cold),
        out_shape=jax.ShapeDtypeStruct((rows, cols), bf16),
        in_specs=[pl.BlockSpec(memory_space=pl.ANY)] * 10,
        out_specs=pl.BlockSpec(memory_space=pltpu.VMEM),
        scratch_shapes=scratch,
        compiler_params=pltpu.CompilerParams(
            collective_id=0, has_side_effects=True, vmem_limit_bytes=60 * 1024 * 1024
        ),
        name="decode_step",
    )(*args[:-1], block_mask.T)


def solution(mesh):
    return jax.shard_map(
        functools.partial(body, mesh.shape["hot"], mesh.shape["cold"]),
        mesh=mesh,
        in_specs=(
            P("cold", "hot"),
            P("hot", "cold"),
            P("hot", "cold"),
            P("cold", "hot"),
            P("hot", "cold"),
            P("hot", "cold"),
            P("cold", "hot"),
            P(),
            P(),
            P(),
        ),
        out_specs=P("cold", "hot"),
        check_vma=False,
    )
```

time: 34.4 us -> 33.9 us (0.985)
  Pallas kernels: 32.8 us -> 32.2 us
    pallas_call x1, Pallas kernels: 32.8 us -> 32.2 us  [body(): pl.pallas_call(functools.partial(kernel, n_hot, n_cold), out_shape=jax.Sh...]
where the time goes in v3:
time: 33.9 us; the launch traced here: 33.7 us
  Pallas kernels  32.2 us (95%)
  local copies, waits for them, and re-layouts  1.47 us (4%)
    pallas_call x1, Pallas kernels, body(): pl.pallas_call(functools.partial(kernel, n_hot, n_cold), out_shape=jax.Sh...  32.2 us
    unnamed x1, local copies, waits for them, and re-layouts  1.47 us

profile of v3, /device:TPU:0, one launch (start us, length us, event | category | flops | bytes accessed | tf_op | source)
XLA Modules:
  0.0 33.7 jit_solution(13191368752458317658)
XLA Ops:
  0.0 32.2 %decode_step.1 = bf16[16,2048]{1,0:T(8,128)(2,1)} custom-call(bf16[16,2048]{1,0:T(8,128)(2,1)} %tok_in.1, bf16[2048,128]{1,0:T(8,128)(2,1)} %hg_in.1, bf16[2048,128]{1,0:T(8,128)(2,1)} %hu_in.1, bf16[128,2048]{1,0:T(8,128)(2,1)} %hd_in.1, bf16[2048,768]{1,0:T(8,128)(2,1)} %cg_in.1, bf16[2048,768]{1,0:T(8,128)(2,1)} %cu_in.1, bf16[768,2048]{1,0:T(8,128)(2,1)} %cd_in.1, ...), custom_call_target="tpu_custom_call" | custom-call | tf_op jit(solution)/shard_map/decode_step/pallas_call | solution.py:354
  32.2 1.5 %copy.12 = bf16[16,2048]{1,0:T(8,128)(2,1)} copy(bf16[16,2048]{1,0:T(8,128)(2,1)} %decode_step.1) | data formatting | bytes 131072

commit v4 on v2

--- a/solution.py
+++ b/solution.py
@@ -9,7 +9,7 @@
 
 BLOCK = 128
 CHUNK = 256
-OUT_CHUNK = 512
+OUT_CHUNK = 1024
 MESH = pl.DeviceIdType.MESH
 NT = (((1,), (1,)), ((), ()))
 SUM_TYPE = jnp.bfloat16
@@ -80,17 +80,17 @@
     load(hid_in, hot_ids)
     load(cid_in, cold_ids)
     load(mask_in, mask)
-    load(hg_in, w_hot.at[:, pl.ds(0, hot_width)])
-    load(hu_in, w_hot.at[:, pl.ds(hot_width, hot_width)])
-    for k in range(chunks):
-        load(cg_in.at[:, pl.ds(k * CHUNK, CHUNK)], w_cold.at[k, :, pl.ds(0, CHUNK)])
-        load(cu_in.at[:, pl.ds(k * CHUNK, CHUNK)], w_cold.at[k, :, pl.ds(CHUNK, CHUNK)])
-    load(hd_in, w_down.at[pl.ds(0, hot_width)])
-    load(cd_in, w_down.at[pl.ds(hot_width, cold_width)])
-
     barrier = pltpu.get_barrier_semaphore()
-    hot_peers = [lax.rem(me_hot + k, n_hot) for k in range(1, n_hot)]
-    pair_peers = [lax.rem(my_pair + k, pairs) for k in range(1, pairs)]
+    way = 2 * (me_hot // (n_hot // 2)) - 1
+    hot_peers = [lax.rem(me_hot + way * k + n_hot, n_hot) for k in range(1, n_hot)]
+    span = pairs // 2
+    my_half, my_place = my_pair // span, my_pair % span
+    far, near = (1 - my_half) * span, my_half * span
+    pair_peers = [far + lax.rem(my_place + k, span) for k in range(1, span)]
+    pair_peers += [near + lax.rem(my_place + k, span) for k in range(1, span)] + [far + my_place]
+    sources = [far + my_place]
+    sources += [far + lax.rem(my_place + span - k, span) for k in range(1, span)]
+    sources += [near + lax.rem(my_place + span - k, span) for k in range(1, span)]
     for peer in hot_peers:
         pl.semaphore_signal(barrier, inc=1, device_id={"hot": peer}, device_id_type=MESH)
     for peer in pair_peers:
@@ -98,30 +98,6 @@
             barrier, inc=1, device_id={"cold": peer * 2 + my_side}, device_id_type=MESH
         )
     pl.semaphore_signal(barrier, inc=1, device_id={"cold": other}, device_id_type=MESH)
-    pl.semaphore_wait(barrier, n_hot - 1 + pairs - 1 + 1)
-
-    sent = []
-
-    def send(src, dst, s_sem, r_sem, device):
-        copy = pltpu.make_async_remote_copy(
-            src_ref=src, dst_ref=dst, send_sem=s_sem, recv_sem=r_sem,
-            device_id=device, device_id_type=MESH,
-        )
-        copy.start()
-        sent.append(copy)
-
-    def arrive(dst, s_sem, r_sem, device):
-        pltpu.make_async_remote_copy(
-            src_ref=dst, dst_ref=dst, send_sem=s_sem, recv_sem=r_sem,
-            device_id=device, device_id_type=MESH,
-        ).wait_recv()
-
-    tok_load.wait()
-    for k, peer in enumerate(pair_peers):
-        send(own_slot, own_slot, tok_send.at[k], tok_recv.at[my_pair],
-             {"cold": peer * 2 + my_side})
-    send(own_slot, own_slot, fwd_send.at[0], fwd_recv.at[my_pair], {"cold": other})
-
     for copy in loads[:3]:
         copy.wait()
     slots_pad = bits_hot.shape[1]
@@ -162,16 +138,46 @@
     bits_cold[...] = dot_nt(pick, bits_t.astype(jnp.bfloat16))
     bits_hot[...] = dot_nt(eye, bits_t.astype(jnp.bfloat16))
 
+    pl.semaphore_wait(barrier, n_hot - 1 + pairs - 1 + 1)
+
+    sent = []
+
+    def send(src, dst, s_sem, r_sem, device):
+        copy = pltpu.make_async_remote_copy(
+            src_ref=src, dst_ref=dst, send_sem=s_sem, recv_sem=r_sem,
+            device_id=device, device_id_type=MESH,
+        )
+        copy.start()
+        sent.append(copy)
+
+    def arrive(dst, s_sem, r_sem, device):
+        pltpu.make_async_remote_copy(
+            src_ref=dst, dst_ref=dst, send_sem=s_sem, recv_sem=r_sem,
+            device_id=device, device_id_type=MESH,
+        ).wait_recv()
+
+    tok_load.wait()
+    for k, peer in enumerate(pair_peers):
+        send(own_slot, own_slot, tok_send.at[k], tok_recv.at[my_pair],
+             {"cold": peer * 2 + my_side})
+    send(own_slot, own_slot, fwd_send.at[0], fwd_recv.at[my_pair], {"cold": other})
+
+    load(hg_in, w_hot.at[:, pl.ds(0, hot_width)])
+    load(hu_in, w_hot.at[:, pl.ds(hot_width, hot_width)])
+    for k in range(chunks):
+        load(cg_in.at[:, pl.ds(k * CHUNK, CHUNK)], w_cold.at[k, :, pl.ds(0, CHUNK)])
+        load(cu_in.at[:, pl.ds(k * CHUNK, CHUNK)], w_cold.at[k, :, pl.ds(CHUNK, CHUNK)])
+    load(hd_in, w_down.at[pl.ds(0, hot_width)])
+    load(cd_in, w_down.at[pl.ds(hot_width, cold_width)])
+
     def slot_of(device):
         return tok_all.at[pl.ds(pl.multiple_of(device * rows, rows), rows)]
 
-    for k in range(1, pairs):
-        source = lax.rem(my_pair + pairs - k, pairs)
+    for k, source in enumerate(sources, 1):
         slot = slot_of(source * 2 + my_side)
         arrive(slot, tok_send.at[k - 1], tok_recv.at[source], {"cold": source * 2 + my_side})
         send(slot, slot, fwd_send.at[k], fwd_recv.at[source], {"cold": other})
-    for k in range(pairs):
-        source = lax.rem(my_pair + pairs - k, pairs)
+    for k, source in enumerate([my_pair] + sources):
         arrive(slot_of(source * 2 + (1 - my_side)), fwd_send.at[k], fwd_recv.at[source],
                {"cold": other})
 
@@ -248,8 +254,7 @@
     for c in range(out_chunks):
         at = pl.ds(c * OUT_CHUNK, OUT_CHUNK)
         total = mine[my_pair, :, at]
-        for k in range(1, pairs):
-            source = lax.rem(my_pair + pairs - k, pairs)
+        for k, source in enumerate(sources, 1):
             arrive(final_in.at[source, :, at], fin_send.at[c, k - 1], fin_recv.at[c, source],
                    {"cold": source * 2 + my_side})
             total = total + final_in[source, :, at].astype(jnp.float32)

time: 34.4 us -> 33.5 us (0.974)
  Pallas kernels: 32.8 us -> 31.8 us
    pallas_call x1, Pallas kernels: 32.8 us -> 31.8 us  [body(): pl.pallas_call(functools.partial(kernel, n_hot, n_cold), out_shape=jax.Sh...]
where the time goes in v4:
time: 33.5 us; the launch traced here: 33.3 us
  Pallas kernels  31.8 us (95%)
  local copies, waits for them, and re-layouts  1.47 us (4%)
    pallas_call x1, Pallas kernels, body(): pl.pallas_call(functools.partial(kernel, n_hot, n_cold), out_shape=jax.Sh...  31.8 us
    unnamed x1, local copies, waits for them, and re-layouts  1.47 us

profile of v4, /device:TPU:0, one launch (start us, length us, event | category | flops | bytes accessed | tf_op | source)
XLA Modules:
  0.0 33.3 jit_solution(13858032275442549313)
XLA Ops:
  0.0 31.8 %decode_step.1 = bf16[16,2048]{1,0:T(8,128)(2,1)} custom-call(bf16[16,2048]{1,0:T(8,128)(2,1)} %tok_in.1, bf16[2048,128]{1,0:T(8,128)(2,1)} %hg_in.1, bf16[2048,128]{1,0:T(8,128)(2,1)} %hu_in.1, bf16[128,2048]{1,0:T(8,128)(2,1)} %hd_in.1, bf16[2048,768]{1,0:T(8,128)(2,1)} %cg_in.1, bf16[2048,768]{1,0:T(8,128)(2,1)} %cu_in.1, bf16[768,2048]{1,0:T(8,128)(2,1)} %cd_in.1, ...), custom_call_target="tpu_custom_call" | custom-call | tf_op jit(solution)/shard_map/decode_step/pallas_call | solution.py:321
  31.8 1.5 %copy.12 = bf16[16,2048]{1,0:T(8,128)(2,1)} copy(bf16[16,2048]{1,0:T(8,128)(2,1)} %decode_step.1) | data formatting | bytes 131072

commit v5 on v4

--- a/solution.py
+++ b/solution.py
@@ -81,16 +81,8 @@
     load(cid_in, cold_ids)
     load(mask_in, mask)
     barrier = pltpu.get_barrier_semaphore()
-    way = 2 * (me_hot // (n_hot // 2)) - 1
-    hot_peers = [lax.rem(me_hot + way * k + n_hot, n_hot) for k in range(1, n_hot)]
-    span = pairs // 2
-    my_half, my_place = my_pair // span, my_pair % span
-    far, near = (1 - my_half) * span, my_half * span
-    pair_peers = [far + lax.rem(my_place + k, span) for k in range(1, span)]
-    pair_peers += [near + lax.rem(my_place + k, span) for k in range(1, span)] + [far + my_place]
-    sources = [far + my_place]
-    sources += [far + lax.rem(my_place + span - k, span) for k in range(1, span)]
-    sources += [near + lax.rem(my_place + span - k, span) for k in range(1, span)]
+    hot_peers = [lax.rem(me_hot + k, n_hot) for k in range(1, n_hot)]
+    pair_peers = [lax.rem(my_pair + k, pairs) for k in range(1, pairs)]
     for peer in hot_peers:
         pl.semaphore_signal(barrier, inc=1, device_id={"hot": peer}, device_id_type=MESH)
     for peer in pair_peers:
@@ -173,11 +165,13 @@
     def slot_of(device):
         return tok_all.at[pl.ds(pl.multiple_of(device * rows, rows), rows)]
 
-    for k, source in enumerate(sources, 1):
+    for k in range(1, pairs):
+        source = lax.rem(my_pair + pairs - k, pairs)
         slot = slot_of(source * 2 + my_side)
         arrive(slot, tok_send.at[k - 1], tok_recv.at[source], {"cold": source * 2 + my_side})
         send(slot, slot, fwd_send.at[k], fwd_recv.at[source], {"cold": other})
-    for k, source in enumerate([my_pair] + sources):
+    for k in range(pairs):
+        source = lax.rem(my_pair + pairs - k, pairs)
         arrive(slot_of(source * 2 + (1 - my_side)), fwd_send.at[k], fwd_recv.at[source],
                {"cold": other})
 
@@ -254,7 +248,8 @@
     for c in range(out_chunks):
         at = pl.ds(c * OUT_CHUNK, OUT_CHUNK)
         total = mine[my_pair, :, at]
-        for k, source in enumerate(sources, 1):
+        for k in range(1, pairs):
+            source = lax.rem(my_pair + pairs - k, pairs)
             arrive(final_in.at[source, :, at], fin_send.at[c, k - 1], fin_recv.at[c, source],
                    {"cold": source * 2 + my_side})
             total = total + final_in[source, :, at].astype(jnp.float32)

time: 33.5 us -> 32.8 us (0.979)
  Pallas kernels: 31.8 us -> 31.1 us
    pallas_call x1, Pallas kernels: 31.8 us -> 31.1 us  [body(): pl.pallas_call(functools.partial(kernel, n_hot, n_cold), out_shape=jax.Sh...]
where the time goes in v5:
time: 32.8 us; the launch traced here: 32.6 us
  Pallas kernels  31.1 us (95%)
  local copies, waits for them, and re-layouts  1.47 us (4%)
    pallas_call x1, Pallas kernels, body(): pl.pallas_call(functools.partial(kernel, n_hot, n_cold), out_shape=jax.Sh...  31.1 us
    unnamed x1, local copies, waits for them, and re-layouts  1.47 us

profile of v5, /device:TPU:0, one launch (start us, length us, event | category | flops | bytes accessed | tf_op | source)
XLA Modules:
  0.0 32.6 jit_solution(6294601750304807074)
XLA Ops:
  0.0 31.1 %decode_step.1 = bf16[16,2048]{1,0:T(8,128)(2,1)} custom-call(bf16[16,2048]{1,0:T(8,128)(2,1)} %tok_in.1, bf16[2048,128]{1,0:T(8,128)(2,1)} %hg_in.1, bf16[2048,128]{1,0:T(8,128)(2,1)} %hu_in.1, bf16[128,2048]{1,0:T(8,128)(2,1)} %hd_in.1, bf16[2048,768]{1,0:T(8,128)(2,1)} %cg_in.1, bf16[2048,768]{1,0:T(8,128)(2,1)} %cu_in.1, bf16[768,2048]{1,0:T(8,128)(2,1)} %cd_in.1, ...), custom_call_target="tpu_custom_call" | custom-call | tf_op jit(solution)/shard_map/decode_step/pallas_call | solution.py:316
  31.1 1.5 %copy.12 = bf16[16,2048]{1,0:T(8,128)(2,1)} copy(bf16[16,2048]{1,0:T(8,128)(2,1)} %decode_step.1) | data formatting | bytes 131072
